TPU v7x, 32 devices: a whole 2x2x4 slice. The times are simulated.
32 devices in a mesh: south: 2 (over core), east: 4 (over z), down: 2 (over x), ens: 2 (over y).
Axes of the slice: x: 2, y: 2, z: 4, core: 2. Of those that a mesh axis runs over, the one named last changes fastest.
Arguments:
- density: float32 [16, 128, 128, 128], P(('ens', 'south'), 'east', 'down'), parts along dimension 0, may hold values from 0.2 to 1.8
- flow_j: float32 [16, 128, 128, 128], P(('ens', 'south'), 'east', 'down'), parts along dimension 0, may hold values from -0.3 to 0.3
- flow_i: float32 [16, 128, 128, 128], P(('ens', 'south'), 'east', 'down'), parts along dimension 0, may hold values from -0.3 to 0.3
- flow_k: float32 [16, 128, 128, 128], P(('ens', 'south'), 'east', 'down'), parts along dimension 0, may hold values from -0.3 to 0.3
Outputs:
- density_end: float32 [16, 128, 128, 128], P(('ens', 'south'), 'east', 'down'), parts along dimension 0
There are 2 independent parts, one for each index of `ens`. A program takes and returns all parts, laid end to end along the dimension named above; each array names one. Nothing has to cross between parts.
All inputs are finite; a program needn't handle non-finite values.
Results may differ from a plain program's by a relative error of at most 0.00002.
Values sent between devices are 32-bit elements; how exact they have to be, the bound alone decides.
A program may use at most 192 MiB of HBM per device.

v0:
```python
import jax
import jax.numpy as jnp
from jax import lax
from jax.sharding import PartitionSpec as P

STEPS = 3


def padded_2(x, sides, width):
    for axis, dim in sides:
        count, length = (lax.axis_size(axis), x.shape[dim])
        up = [(i, (i + 1) % count) for i in range(count - 1)]
        down = [(j, i) for i, j in up]
        last = lax.slice_in_dim(x, length - width, length, axis=dim)
        initial = lax.slice_in_dim(x, 0, width, axis=dim)
        before = lax.ppermute(last, axis, up)
        after = lax.ppermute(initial, axis, down)
        x = jnp.concatenate([before, x, after], axis=dim)
    return x


def inner_cells(values, dims):
    for dim in dims:
        values = lax.slice_in_dim(values, 1, values.shape[dim] - 1, axis=dim)
    return values


def side_cells(values, dim, start, dims):
    others = [other for other in dims if other != dim]
    values = inner_cells(values, others)
    return lax.slice_in_dim(values, start, start + values.shape[dim] - 2, axis=dim)


def advance(padded, flow_j, flow_i, flow_k):
    middle = inner_cells(padded, (0, 1, 2))
    lower = [side_cells(padded, dim, 0, (0, 1, 2)) for dim in (0, 1, 2)]
    upper = [side_cells(padded, dim, 2, (0, 1, 2)) for dim in (0, 1, 2)]
    slopes = [above - below for above, below in zip(upper, lower)]
    smooth_rate = 0.05
    spread = lower[0] + upper[0] + lower[1] + upper[1] + lower[2] + upper[2] - 6.0 * middle
    return (
        middle - flow_j * slopes[0] - flow_i * slopes[1] - flow_k * slopes[2] + smooth_rate * spread
    )


def per_device(density, flow_j, flow_i, flow_k):
    for step in range(STEPS):
        padded = padded_2(density, (("south", 0), ("east", 1), ("down", 2)), 1)
        density = advance(padded, flow_j, flow_i, flow_k)
    return density


def solution(mesh):
    in_specs = (
        P(("ens", "south"), "east", "down", None),
        P(("ens", "south"), "east", "down", None),
        P(("ens", "south"), "east", "down", None),
        P(("ens", "south"), "east", "down", None),
    )
    out_specs = P(("ens", "south"), "east", "down", None)
    return jax.shard_map(
        per_device, mesh=mesh, in_specs=in_specs, out_specs=out_specs, check_vma=False
    )
```

profile of v0, /device:TPU:0, one launch (start us, length us, event | category | flops | bytes accessed | tf_op | source)
XLA Modules:
  0.0 118.4 jit_solution(15454010434939045153)
XLA Ops:
  0.0 0.0 copy-start.4
  0.0 1.8 %fusion.3 = (f32[1,32,64,128]{3,2,1,0:T(8,128)S(1)}, f32[1,32,64,128]{3,2,1,0:T(8,128)S(1)}) fusion(f32[4,32,64,128]{3,2,1,0:T(8,128)} %param.4), kind=kLoop, calls=%fused_computation.74 | loop fusion | bytes 4194304 | tf_op jit(solution)/shard_map/slice | solution.py:15
  1.8 2.6 %collective-permute-start.1 = (f32[1,32,64,128]{3,2,1,0:T(8,128)S(1)}, f32[1,32,64,128]{3,2,1,0:T(8,128)S(1)}, u32[]{:S(2)}, u32[]{:S(2)}) collective-permute-start(f32[1,32,64,128]{3,2,1,0:T(8,128)S(1)} %get-tuple-element.22), channel_id=1, source_target_pairs={{0,16},{1,17},{2,18},{3,19},{4,20},{5,21},{6,22},{7,23},{8,24},{9,... | collective-permute-start | bytes 3145736 | tf_op jit(solution)/shard_map/ppermute | solution.py:16
  4.4 1.3 %collective-permute-start = (f32[1,32,64,128]{3,2,1,0:T(8,128)S(1)}, f32[1,32,64,128]{3,2,1,0:T(8,128)S(1)}, u32[]{:S(2)}, u32[]{:S(2)}) collective-permute-start(f32[1,32,64,128]{3,2,1,0:T(8,128)S(1)} %get-tuple-element.21), channel_id=1, source_target_pairs={{16,0},{17,1},{18,2},{19,3},{20,4},{21,5},{22,6},{23,7},{24,8},{25... | collective-permute-start | bytes 3145736 | tf_op jit(solution)/shard_map/ppermute | solution.py:17
  5.7 0.9 collective-permute-done.1
  6.6 0.1 constant_dynamic-update-slice_fusion.2
  6.7 0.0 copy-done.4
  6.7 0.6 constant_dynamic-update-slice_fusion.1
  7.3 1.7 %collective-permute-done = f32[1,32,64,128]{3,2,1,0:T(8,128)S(1)} collective-permute-done((f32[1,32,64,128]{3,2,1,0:T(8,128)S(1)}, f32[1,32,64,128]{3,2,1,0:T(8,128)S(1)}, u32[]{:S(2)}, u32[]{:S(2)}) %collective-permute-start) | collective-permute-done | bytes 1048608 | tf_op jit(solution)/shard_map/ppermute | solution.py:17
  9.0 0.1 constant_dynamic-update-slice_fusion
  9.1 0.0 copy-start.3
  9.1 4.3 %collective-permute-start.3 = (f32[6,1,64,128]{3,2,1,0:T(8,128)S(1)}, f32[6,1,64,128]{3,2,1,0:T(8,128)S(1)}, u32[]{:S(2)}, u32[]{:S(2)}) collective-permute-start(f32[6,1,64,128]{3,2,1,0:T(8,128)S(1)} %get-tuple-element.15), channel_id=1, source_target_pairs={{0,4},{4,8},{8,12},{1,5},{5,9},{9,13},{2,6},{6,10},{10,14},{3,7},{... | collective-permute-start | bytes 589832 | tf_op jit(solution)/shard_map/ppermute | solution.py:16
  13.4 1.3 %collective-permute-start.2 = (f32[6,1,64,128]{3,2,1,0:T(8,128)S(1)}, f32[6,1,64,128]{3,2,1,0:T(8,128)S(1)}, u32[]{:S(2)}, u32[]{:S(2)}) collective-permute-start(f32[6,1,64,128]{3,2,1,0:T(8,128)S(1)} %get-tuple-element.16), channel_id=1, source_target_pairs={{4,0},{8,4},{12,8},{5,1},{9,5},{13,9},{6,2},{10,6},{14,10},{7,3},{... | collective-permute-start | bytes 589832 | tf_op jit(solution)/shard_map/ppermute | solution.py:17
  14.7 3.1 %collective-permute-done.3 = f32[6,1,64,128]{3,2,1,0:T(8,128)S(1)} collective-permute-done((f32[6,1,64,128]{3,2,1,0:T(8,128)S(1)}, f32[6,1,64,128]{3,2,1,0:T(8,128)S(1)}, u32[]{:S(2)}, u32[]{:S(2)}) %collective-permute-start.3) | collective-permute-done | bytes 196640 | tf_op jit(solution)/shard_map/ppermute | solution.py:16
  17.9 4.1 %collective-permute-done.2 = f32[6,1,64,128]{3,2,1,0:T(8,128)S(1)} collective-permute-done((f32[6,1,64,128]{3,2,1,0:T(8,128)S(1)}, f32[6,1,64,128]{3,2,1,0:T(8,128)S(1)}, u32[]{:S(2)}, u32[]{:S(2)}) %collective-permute-start.2) | collective-permute-done | bytes 196640 | tf_op jit(solution)/shard_map/ppermute | solution.py:17
  22.0 0.1 pad_maximum_fusion.62
  22.2 1.3 %collective-permute-start.4 = (f32[6,34,1,128]{3,1,2,0:T(8,128)S(1)}, f32[6,34,1,128]{3,1,2,0:T(8,128)S(1)}, u32[]{:S(2)}, u32[]{:S(2)}) collective-permute-start(f32[6,34,1,128]{3,1,2,0:T(8,128)S(1)} %copy.22), channel_id=1, source_target_pairs={{2,0},{3,1},{6,4},{7,5},{10,8},{11,9},{14,12},{15,13},{18,16},{19,... | collective-permute-start | bytes 313352 | tf_op jit(solution)/shard_map/ppermute | solution.py:17
  23.5 4.6 %collective-permute-start.5 = (f32[6,34,1,128]{3,1,2,0:T(8,128)S(1)}, f32[6,34,1,128]{3,1,2,0:T(8,128)S(1)}, u32[]{:S(2)}, u32[]{:S(2)}) collective-permute-start(f32[6,34,1,128]{3,1,2,0:T(8,128)S(1)} %copy.24), channel_id=1, source_target_pairs={{0,2},{1,3},{4,6},{5,7},{8,10},{9,11},{12,14},{13,15},{16,18},{17,... | collective-permute-start | bytes 313352 | tf_op jit(solution)/shard_map/ppermute | solution.py:16
  28.0 0.9 collective-permute-done.4
  28.9 0.8 copy.23
  29.7 0.8 collective-permute-done.5
  30.5 0.0 copy-done.3
  30.5 0.8 copy.25
  31.2 16.5 %multiply_add_fusion.2 = f32[4,32,64,128]{3,2,1,0:T(8,128)S(1)} fusion(f32[4,32,64,128]{3,2,1,0:T(8,128)} %param.4, f32[4,32,64,128]{3,2,1,0:T(8,128)} %param.7, f32[6,34,1,128]{3,2,1,0:T(1,128)} %copy.23, f32[6,1,64,128]{3,2,1,0:T(8,128)S(1)} %collective-permute-done.2, f32[6,32,64,128]{3,2,1,0:T(8,128)} %copy-done.3, ...), kind=kLoop, calls=%fused_computation.48 | loop fusion | flops 29360128 | bytes 29962240 | tf_op jit(solution)/shard_map/add | solution.py:42
  47.8 0.1 fusion.2
  47.9 1.4 %collective-permute-start.7 = (f32[1,32,64,128]{3,2,1,0:T(8,128)S(1)}, f32[1,32,64,128]{3,2,1,0:T(8,128)S(1)}, u32[]{:S(2)}, u32[]{:S(2)}) collective-permute-start(f32[1,32,64,128]{3,2,1,0:T(8,128)S(1)} %get-tuple-element.19), channel_id=1, source_target_pairs={{0,16},{1,17},{2,18},{3,19},{4,20},{5,21},{6,22},{7,23},{8,24},{9,... | collective-permute-start | bytes 3145736 | tf_op jit(solution)/shard_map/ppermute | solution.py:16
  49.3 1.3 %collective-permute-start.6 = (f32[1,32,64,128]{3,2,1,0:T(8,128)S(1)}, f32[1,32,64,128]{3,2,1,0:T(8,128)S(1)}, u32[]{:S(2)}, u32[]{:S(2)}) collective-permute-start(f32[1,32,64,128]{3,2,1,0:T(8,128)S(1)} %get-tuple-element.20), channel_id=1, source_target_pairs={{16,0},{17,1},{18,2},{19,3},{20,4},{21,5},{22,6},{23,7},{24,8},{25... | collective-permute-start | bytes 3145736 | tf_op jit(solution)/shard_map/ppermute | solution.py:17
  50.6 0.9 collective-permute-done.7
  51.5 2.4 %collective-permute-done.6 = f32[1,32,64,128]{3,2,1,0:T(8,128)S(1)} collective-permute-done((f32[1,32,64,128]{3,2,1,0:T(8,128)S(1)}, f32[1,32,64,128]{3,2,1,0:T(8,128)S(1)}, u32[]{:S(2)}, u32[]{:S(2)}) %collective-permute-start.6) | collective-permute-done | bytes 1048608 | tf_op jit(solution)/shard_map/ppermute | solution.py:17
  53.8 0.0 copy-start.1
  53.8 0.0 copy-start.2
  53.9 0.0 copy-start
  53.9 3.9 %collective-permute-start.9 = (f32[6,1,64,128]{3,2,1,0:T(8,128)S(1)}, f32[6,1,64,128]{3,2,1,0:T(8,128)S(1)}, u32[]{:S(2)}, u32[]{:S(2)}) collective-permute-start(f32[6,1,64,128]{3,2,1,0:T(8,128)S(1)} %get-tuple-element.13), channel_id=1, source_target_pairs={{0,4},{4,8},{8,12},{1,5},{5,9},{9,13},{2,6},{6,10},{10,14},{3,7},{... | collective-permute-start | bytes 589832 | tf_op jit(solution)/shard_map/ppermute | solution.py:16
  57.8 1.3 %collective-permute-start.8 = (f32[6,1,64,128]{3,2,1,0:T(8,128)S(1)}, f32[6,1,64,128]{3,2,1,0:T(8,128)S(1)}, u32[]{:S(2)}, u32[]{:S(2)}) collective-permute-start(f32[6,1,64,128]{3,2,1,0:T(8,128)S(1)} %get-tuple-element.14), channel_id=1, source_target_pairs={{4,0},{8,4},{12,8},{5,1},{9,5},{13,9},{6,2},{10,6},{14,10},{7,3},{... | collective-permute-start | bytes 589832 | tf_op jit(solution)/shard_map/ppermute | solution.py:17
  59.1 3.1 %collective-permute-done.9 = f32[6,1,64,128]{3,2,1,0:T(8,128)S(1)} collective-permute-done((f32[6,1,64,128]{3,2,1,0:T(8,128)S(1)}, f32[6,1,64,128]{3,2,1,0:T(8,128)S(1)}, u32[]{:S(2)}, u32[]{:S(2)}) %collective-permute-start.9) | collective-permute-done | bytes 196640 | tf_op jit(solution)/shard_map/ppermute | solution.py:16
  62.2 4.1 %collective-permute-done.8 = f32[6,1,64,128]{3,2,1,0:T(8,128)S(1)} collective-permute-done((f32[6,1,64,128]{3,2,1,0:T(8,128)S(1)}, f32[6,1,64,128]{3,2,1,0:T(8,128)S(1)}, u32[]{:S(2)}, u32[]{:S(2)}) %collective-permute-start.8) | collective-permute-done | bytes 196640 | tf_op jit(solution)/shard_map/ppermute | solution.py:17
  66.3 0.1 pad_maximum_fusion.57
  66.5 1.3 %collective-permute-start.10 = (f32[6,34,1,128]{3,1,2,0:T(8,128)S(1)}, f32[6,34,1,128]{3,1,2,0:T(8,128)S(1)}, u32[]{:S(2)}, u32[]{:S(2)}) collective-permute-start(f32[6,34,1,128]{3,1,2,0:T(8,128)S(1)} %copy.26), channel_id=1, source_target_pairs={{2,0},{3,1},{6,4},{7,5},{10,8},{11,9},{14,12},{15,13},{18,16},{19,... | collective-permute-start | bytes 313352 | tf_op jit(solution)/shard_map/ppermute | solution.py:17
  67.8 4.6 %collective-permute-start.11 = (f32[6,34,1,128]{3,1,2,0:T(8,128)S(1)}, f32[6,34,1,128]{3,1,2,0:T(8,128)S(1)}, u32[]{:S(2)}, u32[]{:S(2)}) collective-permute-start(f32[6,34,1,128]{3,1,2,0:T(8,128)S(1)} %copy.28), channel_id=1, source_target_pairs={{0,2},{1,3},{4,6},{5,7},{8,10},{9,11},{12,14},{13,15},{16,18},{17,... | collective-permute-start | bytes 313352 | tf_op jit(solution)/shard_map/ppermute | solution.py:16
  72.4 0.9 collective-permute-done.10
  73.3 0.1 copy.27
  73.4 1.4 %collective-permute-done.11 = f32[6,34,1,128]{3,1,2,0:T(8,128)S(1)} collective-permute-done((f32[6,34,1,128]{3,1,2,0:T(8,128)S(1)}, f32[6,34,1,128]{3,1,2,0:T(8,128)S(1)}, u32[]{:S(2)}, u32[]{:S(2)}) %collective-permute-start.11) | collective-permute-done | bytes 104480 | tf_op jit(solution)/shard_map/ppermute | solution.py:16
  74.8 0.1 copy.29
  74.9 0.0 copy-done.1
  74.9 0.0 copy-done.2
  74.9 0.0 copy-done
  74.9 8.0 %multiply_add_fusion.1 = f32[4,32,64,128]{3,2,1,0:T(8,128)S(1)} fusion(f32[4,32,64,128]{3,2,1,0:T(8,128)S(1)} %multiply_add_fusion.2, f32[4,32,64,128]{3,2,1,0:T(8,128)S(1)} %copy-done, f32[6,34,1,128]{3,2,1,0:T(1,128)S(1)} %copy.27, f32[6,1,64,128]{3,2,1,0:T(8,128)S(1)} %collective-permute-done.8, f32[1,32,64,128]{3,2,1,0:T(8,128)S(1)} %collective-permute-done.6, ...), kind=kLoop, calls=%fused_computation.47 | loop fusion | flops 37748736 | bytes 23670784 | tf_op jit(solution)/shard_map/add | solution.py:42
  83.0 0.1 fusion.1
  83.1 1.4 %collective-permute-start.13 = (f32[1,32,64,128]{3,2,1,0:T(8,128)S(1)}, f32[1,32,64,128]{3,2,1,0:T(8,128)S(1)}, u32[]{:S(2)}, u32[]{:S(2)}) collective-permute-start(f32[1,32,64,128]{3,2,1,0:T(8,128)S(1)} %get-tuple-element.17), channel_id=1, source_target_pairs={{0,16},{1,17},{2,18},{3,19},{4,20},{5,21},{6,22},{7,23},{8,24},{9,... | collective-permute-start | bytes 3145736 | tf_op jit(solution)/shard_map/ppermute | solution.py:16
  84.5 1.3 %collective-permute-start.12 = (f32[1,32,64,128]{3,2,1,0:T(8,128)S(1)}, f32[1,32,64,128]{3,2,1,0:T(8,128)S(1)}, u32[]{:S(2)}, u32[]{:S(2)}) collective-permute-start(f32[1,32,64,128]{3,2,1,0:T(8,128)S(1)} %get-tuple-element.18), channel_id=1, source_target_pairs={{16,0},{17,1},{18,2},{19,3},{20,4},{21,5},{22,6},{23,7},{24,8},{25... | collective-permute-start | bytes 3145736 | tf_op jit(solution)/shard_map/ppermute | solution.py:17
  85.8 0.9 collective-permute-done.13
  86.7 2.4 %collective-permute-done.12 = f32[1,32,64,128]{3,2,1,0:T(8,128)S(1)} collective-permute-done((f32[1,32,64,128]{3,2,1,0:T(8,128)S(1)}, f32[1,32,64,128]{3,2,1,0:T(8,128)S(1)}, u32[]{:S(2)}, u32[]{:S(2)}) %collective-permute-start.12) | collective-permute-done | bytes 1048608 | tf_op jit(solution)/shard_map/ppermute | solution.py:17
  89.1 3.5 %collective-permute-start.15 = (f32[6,1,64,128]{3,2,1,0:T(8,128)S(1)}, f32[6,1,64,128]{3,2,1,0:T(8,128)S(1)}, u32[]{:S(2)}, u32[]{:S(2)}) collective-permute-start(f32[6,1,64,128]{3,2,1,0:T(8,128)S(1)} %get-tuple-element.11), channel_id=1, source_target_pairs={{0,4},{4,8},{8,12},{1,5},{5,9},{9,13},{2,6},{6,10},{10,14},{3,7},{... | collective-permute-start | bytes 589832 | tf_op jit(solution)/shard_map/ppermute | solution.py:16
  92.6 1.3 %collective-permute-start.14 = (f32[6,1,64,128]{3,2,1,0:T(8,128)S(1)}, f32[6,1,64,128]{3,2,1,0:T(8,128)S(1)}, u32[]{:S(2)}, u32[]{:S(2)}) collective-permute-start(f32[6,1,64,128]{3,2,1,0:T(8,128)S(1)} %get-tuple-element.12), channel_id=1, source_target_pairs={{4,0},{8,4},{12,8},{5,1},{9,5},{13,9},{6,2},{10,6},{14,10},{7,3},{... | collective-permute-start | bytes 589832 | tf_op jit(solution)/shard_map/ppermute | solution.py:17
  93.9 3.1 %collective-permute-done.15 = f32[6,1,64,128]{3,2,1,0:T(8,128)S(1)} collective-permute-done((f32[6,1,64,128]{3,2,1,0:T(8,128)S(1)}, f32[6,1,64,128]{3,2,1,0:T(8,128)S(1)}, u32[]{:S(2)}, u32[]{:S(2)}) %collective-permute-start.15) | collective-permute-done | bytes 196640 | tf_op jit(solution)/shard_map/ppermute | solution.py:16
  97.0 4.1 %collective-permute-done.14 = f32[6,1,64,128]{3,2,1,0:T(8,128)S(1)} collective-permute-done((f32[6,1,64,128]{3,2,1,0:T(8,128)S(1)}, f32[6,1,64,128]{3,2,1,0:T(8,128)S(1)}, u32[]{:S(2)}, u32[]{:S(2)}) %collective-permute-start.14) | collective-permute-done | bytes 196640 | tf_op jit(solution)/shard_map/ppermute | solution.py:17
  101.1 0.1 pad_maximum_fusion.52
  101.3 1.3 %collective-permute-start.16 = (f32[6,34,1,128]{3,1,2,0:T(8,128)S(1)}, f32[6,34,1,128]{3,1,2,0:T(8,128)S(1)}, u32[]{:S(2)}, u32[]{:S(2)}) collective-permute-start(f32[6,34,1,128]{3,1,2,0:T(8,128)S(1)} %copy.30), channel_id=1, source_target_pairs={{2,0},{3,1},{6,4},{7,5},{10,8},{11,9},{14,12},{15,13},{18,16},{19,... | collective-permute-start | bytes 313352 | tf_op jit(solution)/shard_map/ppermute | solution.py:17
  102.6 4.6 %collective-permute-start.17 = (f32[6,34,1,128]{3,1,2,0:T(8,128)S(1)}, f32[6,34,1,128]{3,1,2,0:T(8,128)S(1)}, u32[]{:S(2)}, u32[]{:S(2)}) collective-permute-start(f32[6,34,1,128]{3,1,2,0:T(8,128)S(1)} %copy.32), channel_id=1, source_target_pairs={{0,2},{1,3},{4,6},{5,7},{8,10},{9,11},{12,14},{13,15},{16,18},{17,... | collective-permute-start | bytes 313352 | tf_op jit(solution)/shard_map/ppermute | solution.py:16
  107.2 0.9 collective-permute-done.16
  108.1 0.1 copy.31
  108.2 1.4 %collective-permute-done.17 = f32[6,34,1,128]{3,1,2,0:T(8,128)S(1)} collective-permute-done((f32[6,34,1,128]{3,1,2,0:T(8,128)S(1)}, f32[6,34,1,128]{3,1,2,0:T(8,128)S(1)}, u32[]{:S(2)}, u32[]{:S(2)}) %collective-permute-start.17) | collective-permute-done | bytes 104480 | tf_op jit(solution)/shard_map/ppermute | solution.py:16
  109.6 0.1 copy.33
  109.7 8.7 %multiply_add_fusion = f32[4,32,64,128]{3,2,1,0:T(8,128)} fusion(f32[4,32,64,128]{3,2,1,0:T(8,128)S(1)} %multiply_add_fusion.1, f32[4,32,64,128]{3,2,1,0:T(8,128)S(1)} %copy-done, f32[6,34,1,128]{3,2,1,0:T(1,128)S(1)} %copy.31, f32[6,1,64,128]{3,2,1,0:T(8,128)S(1)} %collective-permute-done.14, f32[1,32,64,128]{3,2,1,0:T(8,128)S(1)} %collective-permute-done.12, ...), kind=kLoop, calls=%fused_computation.46 | loop fusion | flops 37748736 | bytes 23670784 | tf_op jit(solution)/shard_map/add | solution.py:42
  (9 shorter events, 0.1 us)
Async XLA Ops:
  0.0 6.7 %copy-start.4 = (f32[4,32,64,128]{3,2,1,0:T(8,128)S(1)}, f32[4,32,64,128]{3,2,1,0:T(8,128)}, u32[]{:S(2)}) copy-start(f32[4,32,64,128]{3,2,1,0:T(8,128)} %param.4) | copy-start | bytes 12582916
  1.8 4.8 %collective-permute-start.1 = (f32[1,32,64,128]{3,2,1,0:T(8,128)S(1)}, f32[1,32,64,128]{3,2,1,0:T(8,128)S(1)}, u32[]{:S(2)}, u32[]{:S(2)}) collective-permute-start(f32[1,32,64,128]{3,2,1,0:T(8,128)S(1)} %get-tuple-element.22), channel_id=1, source_target_pairs={{0,16},{1,17},{2,18},{3,19},{4,20},{5,21},{6,22},{7,23},{8,24},{9,... | collective-permute-start | bytes 3145736 | tf_op jit(solution)/shard_map/ppermute | solution.py:16
  4.4 4.6 %collective-permute-start = (f32[1,32,64,128]{3,2,1,0:T(8,128)S(1)}, f32[1,32,64,128]{3,2,1,0:T(8,128)S(1)}, u32[]{:S(2)}, u32[]{:S(2)}) collective-permute-start(f32[1,32,64,128]{3,2,1,0:T(8,128)S(1)} %get-tuple-element.21), channel_id=1, source_target_pairs={{16,0},{17,1},{18,2},{19,3},{20,4},{21,5},{22,6},{23,7},{24,8},{25... | collective-permute-start | bytes 3145736 | tf_op jit(solution)/shard_map/ppermute | solution.py:17
  9.1 21.4 %copy-start.3 = (f32[6,32,64,128]{3,2,1,0:T(8,128)}, f32[6,32,64,128]{3,2,1,0:T(8,128)S(1)}, u32[]{:S(2)}) copy-start(f32[6,32,64,128]{3,2,1,0:T(8,128)S(1)} %constant_dynamic-update-slice_fusion) | copy-start | bytes 18874372
  9.1 8.8 %collective-permute-start.3 = (f32[6,1,64,128]{3,2,1,0:T(8,128)S(1)}, f32[6,1,64,128]{3,2,1,0:T(8,128)S(1)}, u32[]{:S(2)}, u32[]{:S(2)}) collective-permute-start(f32[6,1,64,128]{3,2,1,0:T(8,128)S(1)} %get-tuple-element.15), channel_id=1, source_target_pairs={{0,4},{4,8},{8,12},{1,5},{5,9},{9,13},{2,6},{6,10},{10,14},{3,7},{... | collective-permute-start | bytes 589832 | tf_op jit(solution)/shard_map/ppermute | solution.py:16
  13.4 8.6 %collective-permute-start.2 = (f32[6,1,64,128]{3,2,1,0:T(8,128)S(1)}, f32[6,1,64,128]{3,2,1,0:T(8,128)S(1)}, u32[]{:S(2)}, u32[]{:S(2)}) collective-permute-start(f32[6,1,64,128]{3,2,1,0:T(8,128)S(1)} %get-tuple-element.16), channel_id=1, source_target_pairs={{4,0},{8,4},{12,8},{5,1},{9,5},{13,9},{6,2},{10,6},{14,10},{7,3},{... | collective-permute-start | bytes 589832 | tf_op jit(solution)/shard_map/ppermute | solution.py:17
  22.2 6.8 %collective-permute-start.4 = (f32[6,34,1,128]{3,1,2,0:T(8,128)S(1)}, f32[6,34,1,128]{3,1,2,0:T(8,128)S(1)}, u32[]{:S(2)}, u32[]{:S(2)}) collective-permute-start(f32[6,34,1,128]{3,1,2,0:T(8,128)S(1)} %copy.22), channel_id=1, source_target_pairs={{2,0},{3,1},{6,4},{7,5},{10,8},{11,9},{14,12},{15,13},{18,16},{19,... | collective-permute-start | bytes 313352 | tf_op jit(solution)/shard_map/ppermute | solution.py:17
  23.5 7.0 %collective-permute-start.5 = (f32[6,34,1,128]{3,1,2,0:T(8,128)S(1)}, f32[6,34,1,128]{3,1,2,0:T(8,128)S(1)}, u32[]{:S(2)}, u32[]{:S(2)}) collective-permute-start(f32[6,34,1,128]{3,1,2,0:T(8,128)S(1)} %copy.24), channel_id=1, source_target_pairs={{0,2},{1,3},{4,6},{5,7},{8,10},{9,11},{12,14},{13,15},{16,18},{17,... | collective-permute-start | bytes 313352 | tf_op jit(solution)/shard_map/ppermute | solution.py:16
  47.9 3.6 %collective-permute-start.7 = (f32[1,32,64,128]{3,2,1,0:T(8,128)S(1)}, f32[1,32,64,128]{3,2,1,0:T(8,128)S(1)}, u32[]{:S(2)}, u32[]{:S(2)}) collective-permute-start(f32[1,32,64,128]{3,2,1,0:T(8,128)S(1)} %get-tuple-element.19), channel_id=1, source_target_pairs={{0,16},{1,17},{2,18},{3,19},{4,20},{5,21},{6,22},{7,23},{8,24},{9,... | collective-permute-start | bytes 3145736 | tf_op jit(solution)/shard_map/ppermute | solution.py:16
  49.3 4.6 %collective-permute-start.6 = (f32[1,32,64,128]{3,2,1,0:T(8,128)S(1)}, f32[1,32,64,128]{3,2,1,0:T(8,128)S(1)}, u32[]{:S(2)}, u32[]{:S(2)}) collective-permute-start(f32[1,32,64,128]{3,2,1,0:T(8,128)S(1)} %get-tuple-element.20), channel_id=1, source_target_pairs={{16,0},{17,1},{18,2},{19,3},{20,4},{21,5},{22,6},{23,7},{24,8},{25... | collective-permute-start | bytes 3145736 | tf_op jit(solution)/shard_map/ppermute | solution.py:17
  53.8 21.1 %copy-start.1 = (f32[4,32,64,128]{3,2,1,0:T(8,128)S(1)}, f32[4,32,64,128]{3,2,1,0:T(8,128)}, u32[]{:S(2)}) copy-start(f32[4,32,64,128]{3,2,1,0:T(8,128)} %param.6) | copy-start | bytes 12582916
  53.8 21.1 %copy-start.2 = (f32[4,32,64,128]{3,2,1,0:T(8,128)S(1)}, f32[4,32,64,128]{3,2,1,0:T(8,128)}, u32[]{:S(2)}) copy-start(f32[4,32,64,128]{3,2,1,0:T(8,128)} %param.5) | copy-start | bytes 12582916
  53.9 21.1 %copy-start = (f32[4,32,64,128]{3,2,1,0:T(8,128)S(1)}, f32[4,32,64,128]{3,2,1,0:T(8,128)}, u32[]{:S(2)}) copy-start(f32[4,32,64,128]{3,2,1,0:T(8,128)} %param.7) | copy-start | bytes 12582916
  53.9 8.3 %collective-permute-start.9 = (f32[6,1,64,128]{3,2,1,0:T(8,128)S(1)}, f32[6,1,64,128]{3,2,1,0:T(8,128)S(1)}, u32[]{:S(2)}, u32[]{:S(2)}) collective-permute-start(f32[6,1,64,128]{3,2,1,0:T(8,128)S(1)} %get-tuple-element.13), channel_id=1, source_target_pairs={{0,4},{4,8},{8,12},{1,5},{5,9},{9,13},{2,6},{6,10},{10,14},{3,7},{... | collective-permute-start | bytes 589832 | tf_op jit(solution)/shard_map/ppermute | solution.py:16
  57.8 8.6 %collective-permute-start.8 = (f32[6,1,64,128]{3,2,1,0:T(8,128)S(1)}, f32[6,1,64,128]{3,2,1,0:T(8,128)S(1)}, u32[]{:S(2)}, u32[]{:S(2)}) collective-permute-start(f32[6,1,64,128]{3,2,1,0:T(8,128)S(1)} %get-tuple-element.14), channel_id=1, source_target_pairs={{4,0},{8,4},{12,8},{5,1},{9,5},{13,9},{6,2},{10,6},{14,10},{7,3},{... | collective-permute-start | bytes 589832 | tf_op jit(solution)/shard_map/ppermute | solution.py:17
  66.5 6.8 %collective-permute-start.10 = (f32[6,34,1,128]{3,1,2,0:T(8,128)S(1)}, f32[6,34,1,128]{3,1,2,0:T(8,128)S(1)}, u32[]{:S(2)}, u32[]{:S(2)}) collective-permute-start(f32[6,34,1,128]{3,1,2,0:T(8,128)S(1)} %copy.26), channel_id=1, source_target_pairs={{2,0},{3,1},{6,4},{7,5},{10,8},{11,9},{14,12},{15,13},{18,16},{19,... | collective-permute-start | bytes 313352 | tf_op jit(solution)/shard_map/ppermute | solution.py:17
  67.8 7.0 %collective-permute-start.11 = (f32[6,34,1,128]{3,1,2,0:T(8,128)S(1)}, f32[6,34,1,128]{3,1,2,0:T(8,128)S(1)}, u32[]{:S(2)}, u32[]{:S(2)}) collective-permute-start(f32[6,34,1,128]{3,1,2,0:T(8,128)S(1)} %copy.28), channel_id=1, source_target_pairs={{0,2},{1,3},{4,6},{5,7},{8,10},{9,11},{12,14},{13,15},{16,18},{17,... | collective-permute-start | bytes 313352 | tf_op jit(solution)/shard_map/ppermute | solution.py:16
  83.1 3.6 %collective-permute-start.13 = (f32[1,32,64,128]{3,2,1,0:T(8,128)S(1)}, f32[1,32,64,128]{3,2,1,0:T(8,128)S(1)}, u32[]{:S(2)}, u32[]{:S(2)}) collective-permute-start(f32[1,32,64,128]{3,2,1,0:T(8,128)S(1)} %get-tuple-element.17), channel_id=1, source_target_pairs={{0,16},{1,17},{2,18},{3,19},{4,20},{5,21},{6,22},{7,23},{8,24},{9,... | collective-permute-start | bytes 3145736 | tf_op jit(solution)/shard_map/ppermute | solution.py:16
  84.5 4.6 %collective-permute-start.12 = (f32[1,32,64,128]{3,2,1,0:T(8,128)S(1)}, f32[1,32,64,128]{3,2,1,0:T(8,128)S(1)}, u32[]{:S(2)}, u32[]{:S(2)}) collective-permute-start(f32[1,32,64,128]{3,2,1,0:T(8,128)S(1)} %get-tuple-element.18), channel_id=1, source_target_pairs={{16,0},{17,1},{18,2},{19,3},{20,4},{21,5},{22,6},{23,7},{24,8},{25... | collective-permute-start | bytes 3145736 | tf_op jit(solution)/shard_map/ppermute | solution.py:17
  89.1 7.9 %collective-permute-start.15 = (f32[6,1,64,128]{3,2,1,0:T(8,128)S(1)}, f32[6,1,64,128]{3,2,1,0:T(8,128)S(1)}, u32[]{:S(2)}, u32[]{:S(2)}) collective-permute-start(f32[6,1,64,128]{3,2,1,0:T(8,128)S(1)} %get-tuple-element.11), channel_id=1, source_target_pairs={{0,4},{4,8},{8,12},{1,5},{5,9},{9,13},{2,6},{6,10},{10,14},{3,7},{... | collective-permute-start | bytes 589832 | tf_op jit(solution)/shard_map/ppermute | solution.py:16
  92.6 8.6 %collective-permute-start.14 = (f32[6,1,64,128]{3,2,1,0:T(8,128)S(1)}, f32[6,1,64,128]{3,2,1,0:T(8,128)S(1)}, u32[]{:S(2)}, u32[]{:S(2)}) collective-permute-start(f32[6,1,64,128]{3,2,1,0:T(8,128)S(1)} %get-tuple-element.12), channel_id=1, source_target_pairs={{4,0},{8,4},{12,8},{5,1},{9,5},{13,9},{6,2},{10,6},{14,10},{7,3},{... | collective-permute-start | bytes 589832 | tf_op jit(solution)/shard_map/ppermute | solution.py:17
  101.3 6.8 %collective-permute-start.16 = (f32[6,34,1,128]{3,1,2,0:T(8,128)S(1)}, f32[6,34,1,128]{3,1,2,0:T(8,128)S(1)}, u32[]{:S(2)}, u32[]{:S(2)}) collective-permute-start(f32[6,34,1,128]{3,1,2,0:T(8,128)S(1)} %copy.30), channel_id=1, source_target_pairs={{2,0},{3,1},{6,4},{7,5},{10,8},{11,9},{14,12},{15,13},{18,16},{19,... | collective-permute-start | bytes 313352 | tf_op jit(solution)/shard_map/ppermute | solution.py:17
  102.6 7.0 %collective-permute-start.17 = (f32[6,34,1,128]{3,1,2,0:T(8,128)S(1)}, f32[6,34,1,128]{3,1,2,0:T(8,128)S(1)}, u32[]{:S(2)}, u32[]{:S(2)}) collective-permute-start(f32[6,34,1,128]{3,1,2,0:T(8,128)S(1)} %copy.32), channel_id=1, source_target_pairs={{0,2},{1,3},{4,6},{5,7},{8,10},{9,11},{12,14},{13,15},{16,18},{17,... | collective-permute-start | bytes 313352 | tf_op jit(solution)/shard_map/ppermute | solution.py:16
where the time goes:
time: 119 us; the launch traced here: 118 us
  starting transfers between devices  42.3 us (36%)
  waiting for transfers between devices  37.1 us (31%)
  other arithmetic  33.8 us (28%)
  local copies, waits for them, and re-layouts  4.86 us (4%)
    add x3, other arithmetic, advance(): middle - flow_j * slopes[0] - flow_i * slopes[1] - flow_k * slopes[2]  33.3 us
    ppermute x9, starting transfers between devices, padded_2(): before = lax.ppermute(last, axis, up)  30.6 us
    ppermute x9, waiting for transfers between devices, padded_2(): after = lax.ppermute(initial, axis, down)  21.4 us
    ppermute x9, waiting for transfers between devices, padded_2(): before = lax.ppermute(last, axis, up)  15.7 us
    ppermute x9, starting transfers between devices, padded_2(): after = lax.ppermute(initial, axis, down)  11.6 us
  transfers between devices with their start and end apart: 18, of which 18 were waited for; matrix products, arithmetic and copies ran while one was open for 1% of the time, Pallas kernels for 0%

commit v1 on v0

v1 whole, which is shorter than its diff:
```python
import functools

import jax
import jax.numpy as jnp
from jax import lax
from jax.experimental import pallas as pl
from jax.experimental.pallas import tpu as pltpu
from jax.sharding import PartitionSpec as P

STEPS = 3
TILE = 8
MESH = pl.DeviceIdType.MESH


def divisor(total, most):
    return max(d for d in range(1, most + 1) if total % d == 0)


def kernel(
    counts, density, flow_j, flow_i, flow_k, out,
    field, fj, fi, fk, pack, land,
    load_sem, flow_sem, isend, irecv, ksend, krecv, jsend, jrecv,
):
    nj, ni, nk, lanes = density.shape
    n_south, n_east, n_down = counts
    south, east, down = (lax.axis_index(a) for a in ("south", "east", "down"))
    has = {
        ("south", 0): (n_south > 1, south > 0),
        ("south", 1): (n_south > 1, south < n_south - 1),
        ("east", 0): (n_east > 1, east > 0),
        ("east", 1): (n_east > 1, east < n_east - 1),
        ("down", 0): (n_down > 1, down > 0),
        ("down", 1): (n_down > 1, down < n_down - 1),
    }
    index = {"south": south, "east": east, "down": down}

    def neighbour(axis, side):
        return {axis: index[axis] + (1 if side else -1)}

    def when_has(axis, side, act):
        static, dynamic = has[axis, side]
        if static:
            pl.when(dynamic)(act)

    def when_edge(axis, side, act):
        static, dynamic = has[axis, side]
        if static:
            pl.when(jnp.logical_not(dynamic))(act)
        else:
            act()

    middle = [j for j in range(nj) if 0 < j < nj - 1]
    outer = [j for j in range(nj) if not 0 < j < nj - 1]
    inner_order = middle + outer
    inside_k = pl.ds(TILE, nk)

    def load(j):
        return pltpu.make_async_copy(
            density.at[j], field.at[0, j + 1, pl.ds(1, ni), inside_k], load_sem.at[j]
        )

    def load_flow(j, d):
        source, target = ((flow_j, fj), (flow_i, fi), (flow_k, fk))[d]
        return pltpu.make_async_copy(source.at[j], target.at[j], flow_sem.at[d, j])

    for j in outer + middle:
        load(j).start()
    for j in inner_order:
        for d in range(3):
            load_flow(j, d).start()

    barrier = pltpu.get_barrier_semaphore()
    for axis, side in has:
        def greet(axis=axis, side=side):
            pl.semaphore_signal(
                barrier, inc=1, device_id=neighbour(axis, side), device_id_type=MESH
            )
        when_has(axis, side, greet)

    def zero_plane(ref_at):
        def act():
            for s in range(STEPS):
                ref_at(s)
        return act

    for side in range(2):
        def zero_j(s, side=side):
            @pl.loop(0, ni)
            def _(i):
                field[s, (nj + 1) * side, i + 1, inside_k, :] = jnp.zeros((nk, lanes), jnp.float32)

        def zero_i(s, side=side):
            for j in range(nj):
                field[s, j + 1, (ni + 1) * side, inside_k, :] = jnp.zeros((nk, lanes), jnp.float32)

        def zero_k(s, side=side):
            row = TILE + nk if side else TILE - 1
            for j in range(nj):
                @pl.loop(0, ni, unroll=8)
                def _(i):
                    field[s, j + 1, i + 1, pl.ds(row, 1), :] = jnp.zeros((1, lanes), jnp.float32)

        when_edge("south", side, zero_plane(zero_j))
        when_edge("east", side, zero_plane(zero_i))
        when_edge("down", side, zero_plane(zero_k))

    pl.semaphore_wait(barrier, sum(jnp.where(d, 1, 0) for s, d in has.values() if s))

    def copy_i(s, side, j):
        face = ni if side else 1
        halo = 0 if side else ni + 1
        return pltpu.make_async_remote_copy(
            src_ref=field.at[s, j + 1, face, inside_k],
            dst_ref=field.at[s, j + 1, halo, inside_k],
            send_sem=isend.at[s, side, j],
            recv_sem=irecv.at[s, 1 - side, j],
            device_id=neighbour("east", side),
            device_id_type=MESH,
        )

    def copy_k(s, side, j):
        return pltpu.make_async_remote_copy(
            src_ref=pack.at[s, side, j],
            dst_ref=land.at[s, 1 - side, j],
            send_sem=ksend.at[s, side, j],
            recv_sem=krecv.at[s, 1 - side, j],
            device_id=neighbour("down", side),
            device_id_type=MESH,
        )

    def copy_j(s, side):
        face = nj if side else 1
        halo = 0 if side else nj + 1
        return pltpu.make_async_remote_copy(
            src_ref=field.at[s, face, pl.ds(1, ni), inside_k],
            dst_ref=field.at[s, halo, pl.ds(1, ni), inside_k],
            send_sem=jsend.at[s, side],
            recv_sem=jrecv.at[s, 1 - side],
            device_id=neighbour("south", side),
            device_id_type=MESH,
        )

    first = jnp.where(south == 0, 1, 0) if n_south > 1 else 0

    def chunk(t):
        return first * (nj - 1 - t) + (1 - first) * t

    def send_chunk(s, t):
        j = chunk(t)
        for side in range(2):
            when_has("east", side, lambda side=side: copy_i(s, side, j).start())
        if n_south > 1 and t == 0:
            pl.when(south == 0)(lambda: copy_j(s, 1).start())
            pl.when(south > 0)(lambda: copy_j(s, 0).start())
        if n_south > 2 and t == nj - 1:
            pl.when((south > 0) & (south < n_south - 1))(lambda: copy_j(s, 1).start())
        for side in range(2):
            def send_k(side=side):
                row = TILE + nk - 1 if side else TILE
                for i in range(ni):
                    pack[s, side, j, pl.ds(i, 1), :] = field[s, j + 1, i + 1, pl.ds(row, 1), :]
                copy_k(s, side, j).start()
            when_has("down", side, send_k)

    def block(s, j, i, size_i, k, size_k):
        def at(dj, di, dk):
            return field[
                s, j + 1 + dj, pl.ds(i + 1 + di, size_i), pl.ds(TILE + k + dk, size_k), :
            ]

        cells = (j, pl.ds(i, size_i), pl.ds(k, size_k), slice(None))
        lower = [at(-1, 0, 0), at(0, -1, 0), at(0, 0, -1)]
        upper = [at(1, 0, 0), at(0, 1, 0), at(0, 0, 1)]
        total = (lower[0] + upper[0]) + (lower[1] + upper[1]) + (lower[2] + upper[2])
        drift = (
            fj[cells] * (upper[0] - lower[0])
            + fi[cells] * (upper[1] - lower[1])
            + fk[cells] * (upper[2] - lower[2])
        )
        value = (0.7 * at(0, 0, 0) + 0.05 * total) - drift
        if s + 1 < STEPS:
            field[s + 1, j + 1, pl.ds(i + 1, size_i), pl.ds(TILE + k, size_k), :] = value
        else:
            out[cells] = value

    for j in range(nj):
        load(j).wait()
    for t in range(nj):
        send_chunk(0, t)

    wide = divisor(ni - 2, 2)
    tall = divisor(ni - 2, 10)
    for s in range(STEPS):
        for at_j, j in enumerate(inner_order):
            if s == 0:
                for d in range(3):
                    load_flow(j, d).wait()
            if at_j == len(middle):
                for side in range(2):
                    when_has("south", side, lambda side=side: copy_j(s, 1 - side).wait_recv())

            @pl.loop(0, (ni - 2) // wide)
            def _(b, j=j):
                block(s, j, 1 + b * wide, wide, TILE, nk - 2 * TILE)

        for t in range(nj):
            j = chunk(t)
            for side in range(2):
                def unpack(side=side):
                    copy_k(s, 1 - side, j).wait_recv()
                    row = TILE + nk if side else TILE - 1
                    for i in range(ni):
                        field[s, j + 1, i + 1, pl.ds(row, 1), :] = land[s, side, j, pl.ds(i, 1), :]
                when_has("down", side, unpack)

            @pl.loop(0, (ni - 2) // tall)
            def _(b):
                block(s, j, 1 + b * tall, tall, 0, TILE)
                block(s, j, 1 + b * tall, tall, nk - TILE, TILE)

            for side in range(2):
                when_has("east", side, lambda side=side: copy_i(s, 1 - side, j).wait_recv())
            block(s, j, 0, 1, 0, nk)
            block(s, j, ni - 1, 1, 0, nk)
            if s + 1 < STEPS:
                send_chunk(s + 1, t)

    for s in range(STEPS):
        for side in range(2):
            when_has("south", side, lambda side=side: copy_j(s, side).wait_send())
            for j in range(nj):
                when_has("east", side, lambda side=side, j=j: copy_i(s, side, j).wait_send())
                when_has("down", side, lambda side=side, j=j: copy_k(s, side, j).wait_send())


def per_device(counts, density, flow_j, flow_i, flow_k):
    nj, ni, nk, lanes = density.shape
    f32 = jnp.float32
    dma = pltpu.SemaphoreType.DMA
    return pl.pallas_call(
        functools.partial(kernel, counts),
        out_shape=jax.ShapeDtypeStruct(density.shape, f32),
        in_specs=[pl.BlockSpec(memory_space=pl.ANY)] * 4,
        out_specs=pl.BlockSpec(memory_space=pltpu.VMEM),
        scratch_shapes=[
            pltpu.VMEM((STEPS, nj + 2, ni + 2, nk + 2 * TILE, lanes), f32),
            pltpu.VMEM((nj, ni, nk, lanes), f32),
            pltpu.VMEM((nj, ni, nk, lanes), f32),
            pltpu.VMEM((nj, ni, nk, lanes), f32),
            pltpu.VMEM((STEPS, 2, nj, ni, lanes), f32),
            pltpu.VMEM((STEPS, 2, nj, ni, lanes), f32),
            dma((nj,)),
            dma((3, nj)),
            dma((STEPS, 2, nj)),
            dma((STEPS, 2, nj)),
            dma((STEPS, 2, nj)),
            dma((STEPS, 2, nj)),
            dma((STEPS, 2)),
            dma((STEPS, 2)),
        ],
        compiler_params=pltpu.CompilerParams(
            collective_id=0, has_side_effects=True, vmem_limit_bytes=60 * 1024 * 1024
        ),
    )(density, flow_j, flow_i, flow_k)


def solution(mesh):
    spec = P(("ens", "south"), "east", "down", None)
    counts = tuple(mesh.shape[a] for a in ("south", "east", "down"))
    return jax.shard_map(
        functools.partial(per_device, counts),
        mesh=mesh,
        in_specs=(spec,) * 4,
        out_specs=spec,
        check_vma=False,
    )
```

time: 119 us -> 28.1 us (0.24)
  starting transfers between devices: 42.3 us -> 0 us
  waiting for transfers between devices: 37.1 us -> 0 us
  other arithmetic: 33.8 us -> 0 us
  Pallas kernels: 0 us -> 23.1 us
    ppermute x18 -> x0, starting transfers between devices: 42.3 us -> none  [the longest x9 30.6 us: padded_2(): before = lax.ppermute(last, axis, up)]
    ppermute x18 -> x0, waiting for transfers between devices: 37.1 us -> none  [the longest x9 21.4 us: padded_2(): after = lax.ppermute(initial, axis, down)]
    add x3 -> x0, other arithmetic: 33.3 us -> none  [advance(): middle - flow_j * slopes[0] - flow_i * slopes[1] - flow_k * slopes[2]]
    pallas_call x0 -> x1, Pallas kernels: none -> 23.1 us  [per_device(): pl.pallas_call(functools.partial(kernel, counts), out_shape=jax.ShapeDtyp...]
    unnamed x12 -> x1, local copies, waits for them, and re-layouts: 0.67 us -> 4.79 us
    slice x10 -> x0, local copies, waits for them, and re-layouts: 2.19 us -> none  [the longest x4 1.86 us: padded_2(): initial = lax.slice_in_dim(x, 0, width, axis=dim)]
    ppermute x6 -> x0, local copies, waits for them, and re-layouts: 1.93 us -> none  [the longest x3 0.97 us: padded_2(): before = lax.ppermute(last, axis, up)]
  transfers between devices with their start and end apart: 18 -> 0, of which waited for: 18 -> 0; matrix products, arithmetic and copies ran while one was open for 1% -> 0% of each run, Pallas kernels for 0% -> 0%
where the time goes in v1:
time: 28.1 us; the launch traced here: 27.9 us
  Pallas kernels  23.1 us (82%)
  local copies, waits for them, and re-layouts  4.79 us (17%)
    pallas_call x1, Pallas kernels, per_device(): pl.pallas_call(functools.partial(kernel, counts), out_shape=jax.ShapeDtyp...  23.1 us
    unnamed x1, local copies, waits for them, and re-layouts  4.79 us

profile of v1, /device:TPU:0, one launch (start us, length us, event | category | flops | bytes accessed | tf_op | source)
XLA Modules:
  0.0 27.9 jit_solution(8838346094555308957)
XLA Ops:
  0.0 23.1 %shard_map.46 = f32[4,32,64,128]{3,2,1,0:T(8,128)} custom-call(f32[4,32,64,128]{3,2,1,0:T(8,128)} %density.1, f32[4,32,64,128]{3,2,1,0:T(8,128)} %flow_j.1, f32[4,32,64,128]{3,2,1,0:T(8,128)} %flow_i.1, f32[4,32,64,128]{3,2,1,0:T(8,128)} %flow_k.1), custom_call_target="tpu_custom_call" | custom-call | tf_op jit(solution)/shard_map/pallas_call | solution.py:240
  23.1 4.8 %copy.6 = f32[4,32,64,128]{3,2,1,0:T(8,128)} copy(f32[4,32,64,128]{3,2,1,0:T(8,128)} %shard_map.46) | data formatting | bytes 8388608

commit v2 on v1

--- a/solution.py
+++ b/solution.py
@@ -239,7 +239,7 @@
     dma = pltpu.SemaphoreType.DMA
     return pl.pallas_call(
         functools.partial(kernel, counts),
-        out_shape=jax.ShapeDtypeStruct(density.shape, f32),
+        out_shape=pltpu.VMEM(density.shape, f32),
         in_specs=[pl.BlockSpec(memory_space=pl.ANY)] * 4,
         out_specs=pl.BlockSpec(memory_space=pltpu.VMEM),
         scratch_shapes=[
@@ -259,7 +259,7 @@
             dma((STEPS, 2)),
         ],
         compiler_params=pltpu.CompilerParams(
-            collective_id=0, has_side_effects=True, vmem_limit_bytes=60 * 1024 * 1024
+            collective_id=0, has_side_effects=True, vmem_limit_bytes=58 * 1024 * 1024
         ),
     )(density, flow_j, flow_i, flow_k)
 

time: 28.1 us -> 23.4 us (0.83)
  local copies, waits for them, and re-layouts: 4.79 us -> 2.02 us
  Pallas kernels: 23.1 us -> 21.2 us
    unnamed x1, local copies, waits for them, and re-layouts: 4.79 us -> 2.02 us
    pallas_call x1, Pallas kernels: 23.1 us -> 21.2 us  [per_device(): pl.pallas_call(functools.partial(kernel, counts), out_shape=pltpu.VMEM(de...]
where the time goes in v2:
time: 23.4 us; the launch traced here: 23.2 us
  Pallas kernels  21.2 us (91%)
  local copies, waits for them, and re-layouts  2.02 us (9%)
    pallas_call x1, Pallas kernels, per_device(): pl.pallas_call(functools.partial(kernel, counts), out_shape=pltpu.VMEM(de...  21.2 us
    unnamed x1, local copies, waits for them, and re-layouts  2.02 us

profile of v2, /device:TPU:0, one launch (start us, length us, event | category | flops | bytes accessed | tf_op | source)
XLA Modules:
  0.0 23.2 jit_solution(13781374732016042209)
XLA Ops:
  0.0 21.2 %shard_map.46 = f32[4,32,64,128]{3,2,1,0:T(8,128)S(1)} custom-call(f32[4,32,64,128]{3,2,1,0:T(8,128)} %density.1, f32[4,32,64,128]{3,2,1,0:T(8,128)} %flow_j.1, f32[4,32,64,128]{3,2,1,0:T(8,128)} %flow_i.1, f32[4,32,64,128]{3,2,1,0:T(8,128)} %flow_k.1), custom_call_target="tpu_custom_call" | custom-call | tf_op jit(solution)/shard_map/pallas_call | solution.py:240
  21.2 2.0 %copy.6 = f32[4,32,64,128]{3,2,1,0:T(8,128)} copy(f32[4,32,64,128]{3,2,1,0:T(8,128)S(1)} %shard_map.46) | data formatting | bytes 8388608

commit v3 on v2

--- a/solution.py
+++ b/solution.py
@@ -55,19 +55,20 @@
     inside_k = pl.ds(TILE, nk)
 
     def load(j):
+        inner = pl.ds(1, ni - 2)
         return pltpu.make_async_copy(
-            density.at[j], field.at[0, j + 1, pl.ds(1, ni), inside_k], load_sem.at[j]
+            density.at[j, inner], field.at[0, j + 1, pl.ds(2, ni - 2), inside_k], load_sem.at[j]
+        )
+
+    def load_face(side):
+        i = (ni - 1) * side
+        return pltpu.make_async_copy(
+            density.at[:, i], field.at[0, pl.ds(1, nj), i + 1, inside_k], load_sem.at[nj + side]
         )
 
     def load_flow(j, d):
         source, target = ((flow_j, fj), (flow_i, fi), (flow_k, fk))[d]
         return pltpu.make_async_copy(source.at[j], target.at[j], flow_sem.at[d, j])
-
-    for j in outer + middle:
-        load(j).start()
-    for j in inner_order:
-        for d in range(3):
-            load_flow(j, d).start()
 
     barrier = pltpu.get_barrier_semaphore()
     for axis, side in has:
@@ -77,34 +78,10 @@
             )
         when_has(axis, side, greet)
 
-    def zero_plane(ref_at):
-        def act():
-            for s in range(STEPS):
-                ref_at(s)
-        return act
-
     for side in range(2):
-        def zero_j(s, side=side):
-            @pl.loop(0, ni)
-            def _(i):
-                field[s, (nj + 1) * side, i + 1, inside_k, :] = jnp.zeros((nk, lanes), jnp.float32)
-
-        def zero_i(s, side=side):
-            for j in range(nj):
-                field[s, j + 1, (ni + 1) * side, inside_k, :] = jnp.zeros((nk, lanes), jnp.float32)
-
-        def zero_k(s, side=side):
-            row = TILE + nk if side else TILE - 1
-            for j in range(nj):
-                @pl.loop(0, ni, unroll=8)
-                def _(i):
-                    field[s, j + 1, i + 1, pl.ds(row, 1), :] = jnp.zeros((1, lanes), jnp.float32)
-
-        when_edge("south", side, zero_plane(zero_j))
-        when_edge("east", side, zero_plane(zero_i))
-        when_edge("down", side, zero_plane(zero_k))
-
-    pl.semaphore_wait(barrier, sum(jnp.where(d, 1, 0) for s, d in has.values() if s))
+        load_face(side).start()
+    for j in outer + middle:
+        load(j).start()
 
     def copy_i(s, side, j):
         face = ni if side else 1
@@ -145,22 +122,25 @@
     def chunk(t):
         return first * (nj - 1 - t) + (1 - first) * t
 
-    def send_chunk(s, t):
-        j = chunk(t)
+    def send_i(s, j):
         for side in range(2):
             when_has("east", side, lambda side=side: copy_i(s, side, j).start())
+
+    def send_j(s, t):
         if n_south > 1 and t == 0:
             pl.when(south == 0)(lambda: copy_j(s, 1).start())
             pl.when(south > 0)(lambda: copy_j(s, 0).start())
         if n_south > 2 and t == nj - 1:
             pl.when((south > 0) & (south < n_south - 1))(lambda: copy_j(s, 1).start())
+
+    def send_k(s, j):
         for side in range(2):
-            def send_k(side=side):
+            def act(side=side):
                 row = TILE + nk - 1 if side else TILE
                 for i in range(ni):
                     pack[s, side, j, pl.ds(i, 1), :] = field[s, j + 1, i + 1, pl.ds(row, 1), :]
                 copy_k(s, side, j).start()
-            when_has("down", side, send_k)
+            when_has("down", side, act)
 
     def block(s, j, i, size_i, k, size_k):
         def at(dj, di, dk):
@@ -183,10 +163,50 @@
         else:
             out[cells] = value
 
+    pl.semaphore_wait(barrier, sum(jnp.where(d, 1, 0) for s, d in has.values() if s))
+    for side in range(2):
+        load_face(side).wait()
+    for t in range(nj):
+        send_i(0, chunk(t))
+    for j in middle:
+        for d in range(3):
+            load_flow(j, d).start()
     for j in range(nj):
         load(j).wait()
     for t in range(nj):
-        send_chunk(0, t)
+        send_j(0, t)
+    for j in outer:
+        for d in range(3):
+            load_flow(j, d).start()
+    for t in range(nj):
+        send_k(0, chunk(t))
+
+    def zero_plane(ref_at):
+        def act():
+            for s in range(STEPS):
+                ref_at(s)
+        return act
+
+    for side in range(2):
+        def zero_j(s, side=side):
+            @pl.loop(0, ni)
+            def _(i):
+                field[s, (nj + 1) * side, i + 1, inside_k, :] = jnp.zeros((nk, lanes), jnp.float32)
+
+        def zero_i(s, side=side):
+            for j in range(nj):
+                field[s, j + 1, (ni + 1) * side, inside_k, :] = jnp.zeros((nk, lanes), jnp.float32)
+
+        def zero_k(s, side=side):
+            row = TILE + nk if side else TILE - 1
+            for j in range(nj):
+                @pl.loop(0, ni, unroll=8)
+                def _(i):
+                    field[s, j + 1, i + 1, pl.ds(row, 1), :] = jnp.zeros((1, lanes), jnp.float32)
+
+        when_edge("south", side, zero_plane(zero_j))
+        when_edge("east", side, zero_plane(zero_i))
+        when_edge("down", side, zero_plane(zero_k))
 
     wide = divisor(ni - 2, 2)
     tall = divisor(ni - 2, 10)
@@ -213,17 +233,21 @@
                         field[s, j + 1, i + 1, pl.ds(row, 1), :] = land[s, side, j, pl.ds(i, 1), :]
                 when_has("down", side, unpack)
 
-            @pl.loop(0, (ni - 2) // tall)
-            def _(b):
-                block(s, j, 1 + b * tall, tall, 0, TILE)
-                block(s, j, 1 + b * tall, tall, nk - TILE, TILE)
-
             for side in range(2):
                 when_has("east", side, lambda side=side: copy_i(s, 1 - side, j).wait_recv())
             block(s, j, 0, 1, 0, nk)
             block(s, j, ni - 1, 1, 0, nk)
             if s + 1 < STEPS:
-                send_chunk(s + 1, t)
+                send_i(s + 1, j)
+
+            @pl.loop(0, (ni - 2) // tall)
+            def _(b):
+                block(s, j, 1 + b * tall, tall, 0, TILE)
+                block(s, j, 1 + b * tall, tall, nk - TILE, TILE)
+
+            if s + 1 < STEPS:
+                send_j(s + 1, t)
+                send_k(s + 1, j)
 
     for s in range(STEPS):
         for side in range(2):
@@ -249,7 +273,7 @@
             pltpu.VMEM((nj, ni, nk, lanes), f32),
             pltpu.VMEM((STEPS, 2, nj, ni, lanes), f32),
             pltpu.VMEM((STEPS, 2, nj, ni, lanes), f32),
-            dma((nj,)),
+            dma((nj + 2,)),
             dma((3, nj)),
             dma((STEPS, 2, nj)),
             dma((STEPS, 2, nj)),

time: 23.4 us -> 21 us (0.90)
  Pallas kernels: 21.2 us -> 18.8 us
    pallas_call x1, Pallas kernels: 21.2 us -> 18.8 us  [per_device(): pl.pallas_call(functools.partial(kernel, counts), out_shape=pltpu.VMEM(de...]
where the time goes in v3:
time: 21 us; the launch traced here: 20.9 us
  Pallas kernels  18.8 us (90%)
  local copies, waits for them, and re-layouts  2.02 us (10%)
    pallas_call x1, Pallas kernels, per_device(): pl.pallas_call(functools.partial(kernel, counts), out_shape=pltpu.VMEM(de...  18.8 us
    unnamed x1, local copies, waits for them, and re-layouts  2.02 us

profile of v3, /device:TPU:0, one launch (start us, length us, event | category | flops | bytes accessed | tf_op | source)
XLA Modules:
  0.0 20.9 jit_solution(3255495494916648427)
XLA Ops:
  0.0 18.8 %shard_map.46 = f32[4,32,64,128]{3,2,1,0:T(8,128)S(1)} custom-call(f32[4,32,64,128]{3,2,1,0:T(8,128)} %density.1, f32[4,32,64,128]{3,2,1,0:T(8,128)} %flow_j.1, f32[4,32,64,128]{3,2,1,0:T(8,128)} %flow_i.1, f32[4,32,64,128]{3,2,1,0:T(8,128)} %flow_k.1), custom_call_target="tpu_custom_call" | custom-call | tf_op jit(solution)/shard_map/pallas_call | solution.py:264
  18.8 2.0 %copy.6 = f32[4,32,64,128]{3,2,1,0:T(8,128)} copy(f32[4,32,64,128]{3,2,1,0:T(8,128)S(1)} %shard_map.46) | data formatting | bytes 8388608
